TPU v7x, 128 devices: a whole 4x4x4 slice. The times are simulated.
128 devices in a mesh: row: 8 (over y, core), col: 16 (over z, x).
Axes of the slice: x: 4, y: 4, z: 4, core: 2. Of those that a mesh axis runs over, the one named last changes fastest.
Arguments:
- covariance: float32 [16384, 16384], P('row', 'col'), as said below
- weights: float32 [16384], P(('row', 'col')), may hold values from 0.5 to 1
- dual_slacks: float32 [16384], P(('row', 'col')), may hold values from 2.5 to 10
- returns: float32 [16384], P(('row', 'col')), may hold values from -6 to 6
- targets: float32 [256], P('col'), may hold values from 0.5 to 1
- sector_duals: float32 [256], replicated, may hold values from -6 to 6
- lengths: int32 [256], replicated, may hold values from 1 to 1024, 16384 in all
Outputs:
- factored: float32 [16384, 16384], P('row', 'col')
- solved_rhs: float32 [16384], P('row')
- sector_cols: float32 [16384, 256], P('row', 'col')
- sector_resid: float32 [256], P('col')
Inputs may be any that keep to these rules, and one draw needn't show every extreme that they name: `lengths`: lengths sum to 16384. `covariance`: only the lower triangle with the diagonal is read; with the added diagonal the system is positive definite.
All inputs are finite; a program needn't handle non-finite values.
Results may differ from a plain program's by a relative error of at most 0.0003.
Values sent between devices are 32-bit elements; how exact they have to be, the bound alone decides.
No kernel may reach another device: no remote copies, remote signals or barrier semaphores. Data moves between devices by JAX's collectives and lax.ppermute only.
A program may use at most 128 MiB of HBM per device.

v0:
```python
import functools

import jax
import jax.numpy as jnp
from jax import lax
from jax.experimental import pallas as pl
from jax.experimental.pallas import tpu as pltpu
from jax.sharding import Mesh
from jax.sharding import PartitionSpec as P

NB = 128
PANELS = 8
LEAD = NB * PANELS
ROW = ("y", "core")
COL = ("z", "x")
ALL = ROW + COL
SIGMA_GAP = 0.5

NN = (((1,), (0,)), ((), ()))
NT = (((1,), (1,)), ((), ()))


def split2(x):
    hi = x.astype(jnp.bfloat16)
    lo = (x - hi.astype(jnp.float32)).astype(jnp.bfloat16)
    return hi, lo


def dot3(a, b, dims):
    ah, al = a
    bh, bl = b
    f = functools.partial(
        lax.dot_general, dimension_numbers=dims, preferred_element_type=jnp.float32
    )
    return f(ah, bh) + (f(ah, bl) + f(al, bh))


def factor_block(d_ref, r_ref):
    lane = lax.broadcasted_iota(jnp.int32, (8, NB), 1)
    sub = lax.broadcasted_iota(jnp.int32, (8, NB), 0)
    wide = lambda x: jnp.broadcast_to(x, (8, NB))
    for g in range(NB // 8):
        base = 8 * g
        head = d_ref[base : base + 8, :]
        cols = [
            jnp.where(lane == base + k, head, wide(head[:, base + k : base + k + 1])) for k in range(8)
        ]
        out = jnp.zeros((8, NB), jnp.float32)
        scale = jnp.zeros((8, NB), jnp.float32)
        for k in range(8):
            r = lax.rsqrt(wide(cols[k][k : k + 1, :]))
            rp = r * r
            m = jnp.where(sub == k, 0.0, cols[k] * rp)
            here = lane == base + k
            row = jnp.where(here, 1.0, wide(head[k : k + 1, :]))
            out = jnp.where(sub == k, row * r, out)
            scale = jnp.where(sub == k, rp, scale)
            head = jnp.where(here, jnp.where(sub == k, 1.0, 0.0), head) - m * row
            for k2 in range(k + 1, 8):
                cols[k2] = cols[k2] - m * wide(cols[k2][k : k + 1, :])
        r_ref[base : base + 8, :] = out
        head = head * scale
        rows = [wide(head[k : k + 1, :]) for k in range(8)]
        block = (lane >= base) & (lane < base + 8)
        for i in range(g + 1, NB // 8):
            cur = d_ref[8 * i : 8 * i + 8, :]
            t = [wide(cur[:, base + k : base + k + 1]) * rows[k] for k in range(8)]
            t = ((t[0] + t[1]) + (t[2] + t[3])) + ((t[4] + t[5]) + (t[6] + t[7]))
            d_ref[8 * i : 8 * i + 8, :] = jnp.where(block, 0.0, cur) - t


def stacked(pair, axis):
    return jnp.concatenate(pair, axis=axis)


def panel_steps(first, last, panels, diag_ref, l_ref, w_ref, d_ref, r_ref):
    n = panels * NB
    ri = lax.broadcasted_iota(jnp.int32, (NB, NB), 0)
    ci = lax.broadcasted_iota(jnp.int32, (NB, NB), 1)
    f = lambda a, b, dims: lax.dot_general(a, b, dims, preferred_element_type=jnp.float32)

    def step(kb, _):
        at = pl.multiple_of(kb * NB, NB)
        d = w_ref[pl.ds(at, NB), pl.ds(at, NB)]
        added = jnp.where(ri == ci, jnp.broadcast_to(diag_ref[pl.ds(kb, 1), :], (NB, NB)), 0.0)
        d_ref[...] = jnp.where(ri >= ci, d, d.T) + added
        factor_block(d_ref, r_ref)
        both = r_ref[...]
        inv = jnp.where(ri >= ci, both, 0.0)
        up = jnp.where(ri < ci, both, jnp.where(ri == ci, 1.0 / both, 0.0))
        l_ref[pl.ds(at, NB), pl.ds(at, NB)] = up.T
        invs = split2(inv)
        for k in range(first, last):

            @pl.when(kb == k)
            def _():
                lo, hi = k * NB, (k + 1) * NB
                if k:
                    w_ref[lo:hi, :lo] = dot3(invs, split2(w_ref[lo:hi, :lo]), NN)
                w_ref[lo:hi, lo:hi] = inv
                if k < panels - 1:
                    low = dot3(split2(w_ref[hi:, lo:hi]), invs, NT)
                    l_ref[hi:, lo:hi] = low
                    l_ref[lo:hi, hi:] = jnp.zeros((NB, n - hi), jnp.float32)
                    w_ref[lo:hi, hi:] = jnp.zeros((NB, n - hi), jnp.float32)
                    lh, ll = split2(low)
                    both_l, twice_l = stacked((lh, ll), 1), stacked((lh, lh), 1)
                    wh, wl = split2(w_ref[lo:hi, :hi])
                    t = f(both_l, stacked((wh, wh), 0), NN) + f(lh, wl, NN)
                    if k:
                        w_ref[hi:, :lo] -= t[:, :lo]
                    w_ref[hi:, lo:hi] = -t[:, lo:]
                    for c in range(hi, n, 2 * NB):
                        a0, a1 = c - hi, min(c + 2 * NB, n) - hi
                        t = f(both_l[a0:], twice_l[a0:a1], NT) + f(lh[a0:], ll[a0:a1], NT)
                        w_ref[c:, c : hi + a1] -= t

        return 0

    lax.fori_loop(first, last, step, 0)


def chol_start(panels, last, mine_ref, other_ref, diag_ref, l_ref, w_ref, d_ref, r_ref):
    core = lax.axis_index("core")
    span = mine_ref.shape[0]

    @pl.when(core == 0)
    def _():
        w_ref[:span] = mine_ref[...]
        w_ref[span:] = other_ref[...]

    @pl.when(core == 1)
    def _():
        w_ref[:span] = other_ref[...]
        w_ref[span:] = mine_ref[...]

    panel_steps(0, last, panels, diag_ref, l_ref, w_ref, d_ref, r_ref)


def chol_part(kernel, *args):
    n = args[0].shape[1]
    return pl.pallas_call(
        kernel,
        out_shape=[jax.ShapeDtypeStruct((n, n), jnp.float32)] * 2,
        in_specs=[pl.BlockSpec(memory_space=pltpu.VMEM)] * 3,
        out_specs=[pl.BlockSpec(memory_space=pltpu.VMEM)] * 2,
        scratch_shapes=[pltpu.VMEM((NB, NB), jnp.float32)] * 2,
        compiler_params=pltpu.CompilerParams(vmem_limit_bytes=50 * 2**20),
    )(*args)


def flat(y, core, z, x):
    return ((y * 2 + core) * 4 + z) * 4 + x


def factor_kernel(w_ref, own_ref, other_ref, e_ref, xh_ref, xl_ref, g_ref, head_ref, ah, al, mh, ml, acc):
    n, wide = LEAD, 256
    core, y, col = lax.axis_index("core"), lax.axis_index("y"), lax.axis_index(COL)
    piece = own_ref.shape[1]
    for k in range(4):
        group = 2 * lax.rem(y - k + 4, 4)
        for source, q in ((own_ref, core), (other_ref, 1 - core)):
            hi, lo = split2(source[k])
            at = pl.multiple_of((group + q) * piece, piece)
            ah[pl.ds(at, piece), :] = hi
            al[pl.ds(at, piece), :] = lo
    ri = lax.broadcasted_iota(jnp.int32, (wide, n), 0)
    ci = lax.broadcasted_iota(jnp.int32, (wide, n), 1)
    part = lambda i: pl.ds(pl.multiple_of(i * wide, wide), wide)

    def first(i, _):
        acc[...] = jnp.zeros_like(acc)

        def add(k, _):
            w = split2(w_ref[part(i), part(k)])
            acc[:, :n] += dot3(w, (ah[:, part(k)], al[:, part(k)]), NT)
            acc[:, n:] += dot3(w, split2(e_ref[part(k), :]), NN)
            return 0

        lax.fori_loop(0, i + 1, add, 0)
        m = acc[:, :n]
        m = jnp.where(col == 0, jnp.where(ri + i * wide == ci, -1.0, 0.0), m)
        mh[part(i), :n], ml[part(i), :n] = split2(m)
        m = acc[:, n:]
        head_ref[part(i), :] = m
        mh[part(i), n:], ml[part(i), n:] = split2(m)
        return 0

    def second(i, _):
        acc[...] = jnp.zeros_like(acc)

        def add(k, _):
            w = split2(w_ref[part(k), part(i)].T)
            acc[...] += dot3(w, (mh[part(k), :], ml[part(k), :]), NN)
            return 0

        lax.fori_loop(i, n // wide, add, 0)
        xh_ref[part(i), :], xl_ref[part(i), :] = split2(acc[:, :n])
        gh, gl = split2(acc[:, n:])
        g_ref[part(i), :64], g_ref[part(i), 64:] = gh[:, :64], gl[:, :64]
        return 0

    lax.fori_loop(0, n // wide, first, 0)
    lax.fori_loop(0, n // wide, second, 0)


def weigh(inverse, own, other, extra):
    n = inverse.shape[0]
    vmem = pl.BlockSpec(memory_space=pltpu.VMEM)
    return pl.pallas_call(
        factor_kernel,
        out_shape=[
            jax.ShapeDtypeStruct((n, n), jnp.bfloat16),
            jax.ShapeDtypeStruct((n, n), jnp.bfloat16),
            jax.ShapeDtypeStruct((n, NB), jnp.bfloat16),
            jax.ShapeDtypeStruct((n, NB), jnp.float32),
        ],
        in_specs=[vmem] * 4,
        out_specs=[vmem] * 4,
        scratch_shapes=[pltpu.VMEM((n, n), jnp.bfloat16)] * 2
        + [pltpu.VMEM((n, n + NB), jnp.bfloat16)] * 2
        + [pltpu.VMEM((256, n + NB), jnp.float32)],
        compiler_params=pltpu.CompilerParams(vmem_limit_bytes=56 * 2**20),
        name="weigh",
    )(inverse, own, other, extra)


def update_kernel(rows_ref, xh_ref, xl_ref, g_ref, cov_ref, low_ref, e_ref, head_ref, d_ref, out_ref, rhs_ref, sec_ref):
    block, n = rows_ref.shape
    step = pl.program_id(0)
    rows_total = pl.num_programs(0) * block
    row, col = lax.axis_index(ROW), lax.axis_index(COL)
    ah, al = split2(rows_ref[...])
    x = (xh_ref[...], xl_ref[...])
    t = dot3((ah, al), x, NN)
    f = functools.partial(
        lax.dot_general, dimension_numbers=NN, preferred_element_type=jnp.float32
    )
    g = g_ref[...]
    p, q = f(ah, g), f(al, g)
    extra = e_ref[...] - (p[:, :64] + (p[:, 64:] + q[:, :64]))
    top = (row == 0) & (step * block < LEAD)
    extra = jnp.where(top, head_ref[:, :64], extra)
    sec_ref[...] = extra[:, 1 : 1 + sec_ref.shape[1]]
    rhs_ref[...] = jnp.concatenate([extra, jnp.zeros_like(extra)], axis=1).T[0:1, :]
    ri = lax.broadcasted_iota(jnp.int32, (block, n), 0) + (row * rows_total + step * block)
    ci = lax.broadcasted_iota(jnp.int32, (block, n), 1) + col * n
    base = jnp.where(ri == ci, cov_ref[...] + d_ref[...], cov_ref[...])
    base = jnp.where(col == 0, 0.0, base)
    tile = jnp.where(ri >= ci, base - t, 0.0)
    out_ref[...] = jnp.where(top & (col == 0), low_ref[...], tile)


def update(rows, xh, xl, g, covariance, lower, extra, head, diag, sectors):
    m, n = covariance.shape
    block = 512
    last = LEAD // block - 1
    whole = lambda a: pl.BlockSpec(a.shape, lambda i: (0, 0))
    lines = lambda w: pl.BlockSpec((block, w), lambda i: (i, 0))
    ahead = lambda w: pl.BlockSpec((block, w), lambda i: (jnp.minimum(i, last), 0))
    return pl.pallas_call(
        update_kernel,
        grid=(m // block,),
        out_shape=[
            jax.ShapeDtypeStruct((m, n), jnp.float32),
            jax.ShapeDtypeStruct((1, m), jnp.float32),
            jax.ShapeDtypeStruct((m, sectors), jnp.float32),
        ],
        in_specs=[lines(n), whole(xh), whole(xl), whole(g), lines(n), ahead(n), lines(64), ahead(NB), whole(diag)],
        out_specs=[lines(n), pl.BlockSpec((1, block), lambda i: (0, i)), lines(sectors)],
        compiler_params=pltpu.CompilerParams(
            vmem_limit_bytes=56 * 2**20, dimension_semantics=("arbitrary",)
        ),
        name="update",
    )(rows, xh, xl, g, covariance, lower, extra, head, diag)


def place(y, core, near, far):
    return flat(y, core, far, near) if core == 0 else flat(y, core, near, far)


def spread_lead(half, panel):
    first = lax.axis_index("core") == 0
    z, x, y = lax.axis_index("z"), lax.axis_index("x"), lax.axis_index("y")
    near, far = jnp.where(first, x, z), jnp.where(first, z, x)
    four = range(4)
    cores = range(2)
    loads = half.reshape(4, -1, LEAD)
    bundle = loads[0]
    for k in range(1, 4):
        got = lax.ppermute(loads[k], ALL, [(place(0, c, 0, 0), place(0, c, k, 0)) for c in cores])
        bundle = jnp.where(near == k, got, bundle)
    loads = bundle.reshape(4, -1, LEAD)
    part = loads[0]
    for k in range(1, 4):
        pairs = [(place(0, c, n, 0), place(0, c, n, k)) for c in cores for n in four]
        part = jnp.where(far == k, lax.ppermute(loads[k], ALL, pairs), part)
    own = part
    for k in range(1, 4):
        pairs = [(place(0, c, n, f), place(k, c, n, f)) for c in cores for n in four for f in four]
        own = jnp.where(y == k, lax.ppermute(part, ALL, pairs), own)

    def exchange(block, index, ahead):
        out = lax.dynamic_update_slice_in_dim(
            jnp.zeros((4,) + block.shape, block.dtype), block[None], index, 0
        )
        for k in range(1, 4):
            got = lax.ppermute(block, ALL, ahead(k))
            out = lax.dynamic_update_slice_in_dim(out, got[None], lax.rem(index - k + 4, 4), 0)
        return out.reshape(-1, LEAD)

    def along_far(k):
        return [
            (place(v, c, n, f), place(v, c, n, (f + k) % 4)) for v in four for c in cores for n in four for f in four
        ]

    def along_near(k):
        return [
            (place(v, c, n, f), place(v, c, (n + k) % 4, f)) for v in four for c in cores for n in four for f in four
        ]

    own = exchange(own, far, along_far)
    own, panel = lax.optimization_barrier((own, panel))
    return exchange(own, near, along_near), panel


def on_device(covariance, weights, dual_slacks, returns, targets, sector_duals, lengths):
    tile_rows, tile_cols = covariance.shape
    rows_n, cols_n = 8, 16
    order = tile_rows * rows_n
    row_id, col_id = lax.axis_index(ROW), lax.axis_index(COL)
    row_start, col_start = row_id * tile_rows, col_id * tile_cols
    sectors_here = targets.shape[0]
    global_rows = row_start + jnp.arange(tile_rows, dtype=jnp.int32)
    global_cols = col_start + jnp.arange(tile_cols, dtype=jnp.int32)

    panel, small = lax.optimization_barrier(
        (jnp.where(col_id == 0, covariance, 0.0), jnp.stack([weights, dual_slacks, returns]))
    )
    own = lax.psum_scatter(panel, COL, scatter_dimension=0, tiled=True)
    small = lax.all_gather(small, COL, axis=0, tiled=True)
    lower_mask = global_rows[:, None] >= global_cols[None, :]
    strict_mask = global_rows[:, None] > global_cols[None, :]

    half = LEAD // 2
    second = lax.ppermute(covariance[half:LEAD], ALL, [(flat(0, 0, 0, 0), flat(0, 1, 0, 0))])
    mine = jnp.where(lax.axis_index("core") == 0, covariance[:half], second)
    mine, small = lax.optimization_barrier((mine, small))
    mine, own = spread_lead(mine, own)

    small = lax.all_gather(small, ROW, axis=0, tiled=True)
    small = small.reshape(rows_n * cols_n, 3, -1)
    full_weights, full_slacks, full_returns = (small[:, k].reshape(order) for k in range(3))
    weight_rows = lax.dynamic_slice_in_dim(full_weights, row_start, tile_rows)
    weight_cols = lax.dynamic_slice_in_dim(full_weights, col_start, tile_cols)
    row_part = jnp.sum(jnp.where(lower_mask, covariance, 0.0) * weight_cols[None, :], axis=1)
    col_part = jnp.sum(jnp.where(strict_mask, covariance, 0.0) * weight_rows[:, None], axis=0)
    lines = jnp.concatenate([col_part, row_part[:LEAD]]).reshape(1, -1)
    lines = lax.all_gather(lines, ROW, axis=0, tiled=True)
    col_sum, head_part = jnp.sum(lines[:, :tile_cols], axis=0), lines[0, tile_cols:]
    left = row_part[:tile_cols] + jnp.where(col_id == 2 * row_id, col_sum, 0.0)
    right = row_part[tile_cols:] + jnp.where(col_id == 2 * row_id + 1, col_sum, 0.0)
    head_part = head_part + jnp.where(col_id == 0, col_sum, 0.0)
    lines = jnp.concatenate([left, right, head_part]).reshape(1, -1)
    lines = lax.all_gather(lines, COL, axis=0, tiled=True)
    product = jnp.sum(lines, axis=0)

    row_lines = lax.all_gather(own, COL, axis=0, tiled=True)
    moved = lax.ppermute(
        own, ALL, [(g, (g % rows_n) * cols_n + g // rows_n) for g in range(rows_n * cols_n)]
    )
    around = [moved]
    for k in range(1, 4):
        around.append(lax.ppermute(moved, "y", [(v, (v + k) % 4) for v in range(4)]))
    diag = full_slacks / full_weights
    mean_gap = jnp.sum(full_weights * full_slacks) / order

    head_index = jnp.arange(LEAD, dtype=jnp.int32)
    other = lax.ppermute(mine, "core", [(0, 1), (1, 0)])
    head_diag = diag[:LEAD].reshape(PANELS, NB)
    lower, inverse = chol_part(functools.partial(chol_start, PANELS, PANELS), mine, other, head_diag)
    around, inverse = lax.optimization_barrier((jnp.stack(around), inverse))
    across = lax.ppermute(around, "core", [(0, 1), (1, 0)])

    sector_ends = jnp.cumsum(lengths)
    offsets = sector_ends - lengths
    sector_index = col_id * sectors_here + jnp.arange(sectors_here, dtype=jnp.int32)
    my_offsets, my_ends = jnp.take(offsets, sector_index), jnp.take(sector_ends, sector_index)
    my_sizes = jnp.take(lengths, sector_index).astype(jnp.float32)
    assets = jnp.arange(order, dtype=jnp.int32)
    inside = (assets[None, :] >= my_offsets[:, None]) & (assets[None, :] < my_ends[:, None])
    sector_resid = targets - jnp.sum(jnp.where(inside, full_weights[None, :], 0.0), axis=1) / my_sizes

    def extras(index, start, count, product_here):
        member = (index[:, None] >= offsets[None, :]) & (index[:, None] < sector_ends[None, :])
        prices = jnp.sum(jnp.where(member, sector_duals[None, :], 0.0), axis=1)
        w = lax.dynamic_slice_in_dim(full_weights, start, count)
        ret = lax.dynamic_slice_in_dim(full_returns, start, count)
        rhs = ret - product_here - prices + SIGMA_GAP * mean_gap / w
        mine = (index[:, None] >= my_offsets[None, :]) & (index[:, None] < my_ends[None, :])
        sectors = jnp.where(mine, lax.rsqrt(my_sizes)[None, :], 0.0)
        return jnp.concatenate(
            [rhs[:, None], sectors, jnp.zeros((count, 47), jnp.float32)], axis=1
        )

    head = extras(head_index, 0, LEAD, product[tile_rows:])
    body = extras(global_rows, row_start, tile_rows, product[:tile_rows])
    head = jnp.concatenate([head, jnp.zeros_like(head)], axis=1)
    xh, xl, g, solved_head = weigh(inverse, around, across, head)
    diag_cols = lax.dynamic_slice_in_dim(diag, col_start, tile_cols)[None, :]
    factored, rhs, sector_cols = update(
        row_lines, xh, xl, g, covariance, lower, body, solved_head, diag_cols, sectors_here
    )
    return factored, rhs.reshape(tile_rows), sector_cols, sector_resid


def solution(mesh):
    finer = Mesh(mesh.devices.reshape(4, 2, 4, 4), ALL)
    in_specs = (P(ROW, COL), P(ALL), P(ALL), P(ALL), P(COL), P(), P())
    out_specs = (P(ROW, COL), P(ROW), P(ROW, COL), P(COL))
    return jax.shard_map(on_device, mesh=finer, in_specs=in_specs, out_specs=out_specs, check_vma=False)
```

profile of v0, /device:TPU:1, one launch (start us, length us, event | category | flops | bytes accessed | tf_op | source)
XLA Modules:
  0.0 343.6 jit_solution(266309515665903136)
XLA Ops:
  7.3 8.7 %broadcast_select_fusion = f32[2048,1024]{1,0:T(8,128)} fusion(f32[2048,1024]{1,0:T(8,128)} %cov_ref.1, pred[]{:T(512)S(6)} %eq.45), kind=kLoop, calls=%fused_computation.5 | loop fusion | flops 2097152 | bytes 16777216 | tf_op jit(solution)/shard_map/jit(_where)/select_n | solution.py:338
  19.1 19.1 %all-gather.2 = f32[16,3,128]{2,1,0:T(4,128)S(1)} all-gather(f32[1,3,128]{2,1,0:T(4,128)S(1)} %bitcast.70), channel_id=1, replica_groups=mesh['y'=4,'core'=2,'z'=4,'x'=4] {'z','x'}, dimensions={0}, use_global_device_ids=true | all-gather | bytes 26112 | tf_op jit(solution)/shard_map/all_gather | solution.py:341
  38.2 3.0 slice_select_fusion
  42.2 3.1 collective-permute-start.3
  47.5 2.1 collective-permute-start.1
  49.6 12.9 %collective-permute-done.3 = f32[128,1024]{1,0:T(8,128)S(1)} collective-permute-done((f32[128,1024]{1,0:T(8,128)}, f32[128,1024]{1,0:T(8,128)S(1)}, u32[]{:S(2)}, u32[]{:S(2)}) %collective-permute-start.3) | collective-permute-done | bytes 524320 | tf_op jit(solution)/shard_map/ppermute | solution.py:291
  62.6 13.6 %collective-permute-done.2 = f32[128,1024]{1,0:T(8,128)} collective-permute-done((f32[128,1024]{1,0:T(8,128)}, f32[128,1024]{1,0:T(8,128)}, u32[]{:S(2)}, u32[]{:S(2)}) %collective-permute-start.2) | collective-permute-done | bytes 524320 | tf_op jit(solution)/shard_map/ppermute | solution.py:291
  88.3 4.2 %collective-permute-start.11 = (f32[32,1024]{1,0:T(8,128)S(1)}, f32[32,1024]{1,0:T(8,128)S(1)}, u32[]{:S(2)}, u32[]{:S(2)}) collective-permute-start(f32[32,1024]{1,0:T(8,128)S(1)} %get-tuple-element.62), channel_id=1, source_target_pairs={{0,8},{4,12},{8,0},{12,4},{1,9},{5,13},{9,1},{13,5},{2,10},{6,14},... | collective-permute-start | bytes 393224 | tf_op jit(solution)/shard_map/ppermute | solution.py:308
  93.9 6.6 %collective-permute-done.11 = f32[32,1024]{1,0:T(8,128)S(1)} collective-permute-done((f32[32,1024]{1,0:T(8,128)S(1)}, f32[32,1024]{1,0:T(8,128)S(1)}, u32[]{:S(2)}, u32[]{:S(2)}) %collective-permute-start.11) | collective-permute-done | bytes 131104 | tf_op jit(solution)/shard_map/ppermute | solution.py:308
  106.2 15.7 %all_gather.17 = f32[384,128]{1,0:T(8,128)S(1)} all-gather(f32[48,128]{1,0:T(8,128)S(1)} %reshape.141), channel_id=1, replica_groups=mesh['y'=4,'core'=2,'z'=4,'x'=4] {'y','core'}, dimensions={0}, use_global_device_ids=true | all-gather | bytes 221184 | tf_op jit(solution)/shard_map/all_gather | solution.py:351
  122.6 2.2 collective-permute-start.18
  126.4 9.8 %collective-permute-done.17 = f32[128,1024]{1,0:T(8,128)S(1)} collective-permute-done((f32[128,1024]{1,0:T(8,128)S(1)}, f32[128,1024]{1,0:T(8,128)S(1)}, u32[]{:S(2)}, u32[]{:S(2)}) %collective-permute-start.17) | collective-permute-done | bytes 524320 | tf_op jit(solution)/shard_map/ppermute | solution.py:308
  136.2 5.5 %collective-permute-done.18 = f32[128,1024]{1,0:T(8,128)S(1)} collective-permute-done((f32[128,1024]{1,0:T(8,128)S(1)}, f32[128,1024]{1,0:T(8,128)S(1)}, u32[]{:S(2)}, u32[]{:S(2)}) %collective-permute-start.18) | collective-permute-done | bytes 524320 | tf_op jit(solution)/shard_map/ppermute | solution.py:308
  142.2 4.7 %multiply_reduce_fusion = (f32[1024]{0:T(1024)S(1)}, f32[2048]{0:T(1024)S(1)}) fusion(f32[2048,1024]{1,0:T(8,128)} %cov_ref.1, f32[2048]{0:T(1024)S(1)} %dynamic_slice.24, s32[1024]{0:T(1024)S(1)} %iota_add_fusion.1, s32[2048]{0:T(1024)S(1)} %iota_add_fusion, f32[1024]{0:T(1024)S(1)} %get-tuple-element.58), kind=kLoop, calls=%fused_computation.3 | loop fusion | flops 16774144 | bytes 8425472 | tf_op jit(solution)/shard_map/reduce_sum | solution.py:357
  146.9 3.3 collective-permute-start.13
  150.2 34.2 %all-gather = f32[16384]{0:T(1024)S(1)} all-gather(f32[2048]{0:T(1024)S(1)} %pad_maximum_fusion.2), channel_id=2, replica_groups=mesh['y'=4,'core'=2,'z'=4,'x'=4] {'y','core'}, dimensions={0}, use_global_device_ids=true | all-gather | bytes 73728 | tf_op jit(solution)/shard_map/all_gather | solution.py:359
  184.5 17.8 %all-gather.1 = f32[49152]{0:T(1024)S(1)} all-gather(f32[3072]{0:T(1024)S(1)} %pad_maximum_fusion.1), channel_id=3, replica_groups=mesh['y'=4,'core'=2,'z'=4,'x'=4] {'z','x'}, dimensions={0}, use_global_device_ids=true | all-gather | bytes 208896 | tf_op jit(solution)/shard_map/all_gather | solution.py:365
  205.7 7.1 %collective-permute-done.16 = f32[128,1024]{1,0:T(8,128)S(1)} collective-permute-done((f32[128,1024]{1,0:T(8,128)}, f32[128,1024]{1,0:T(8,128)S(1)}, u32[]{:S(2)}, u32[]{:S(2)}) %collective-permute-start.16) | collective-permute-done | bytes 524320 | tf_op jit(solution)/shard_map/ppermute | solution.py:374
  214.8 15.5 %collective-permute-done.14 = f32[128,1024]{1,0:T(8,128)} collective-permute-done((f32[128,1024]{1,0:T(8,128)}, f32[128,1024]{1,0:T(8,128)}, u32[]{:S(2)}, u32[]{:S(2)}) %collective-permute-start.14) | collective-permute-done | bytes 524320 | tf_op jit(solution)/shard_map/ppermute | solution.py:374
  230.3 2.9 pad_maximum_fusion.own_ref
  233.2 45.6 %shard_map.102 = (f32[1024,1024]{1,0:T(8,128)}, f32[1024,1024]{1,0:T(8,128)}) custom-call(f32[512,1024]{1,0:T(8,128)S(1)} %bitcast.47, f32[512,1024]{1,0:T(8,128)} %collective-permute-done.20.other_ref, f32[8,128]{1,0:T(8,128)S(1)} %fusion.10.diag_ref), custom_call_target="tpu_custom_call" | custom-call | tf_op jit(solution)/shard_map/pallas_call | solution.py:142
  286.9 24.1 %weigh.1 = (bf16[1024,1024]{1,0:T(8,128)(2,1)}, bf16[1024,1024]{1,0:T(8,128)(2,1)}, bf16[1024,128]{1,0:T(8,128)(2,1)}, f32[1024,128]{1,0:T(8,128)}) custom-call(f32[1024,1024]{1,0:T(8,128)} %get-tuple-element.29.w_ref, f32[4,128,1024]{2,1,0:T(8,128)} %pad_maximum_fusion.own_ref, f32[4,128,1024]{2,1,0:T(8,128)} %copy-done.1, ...), custom_call_target="tpu_custom_call" | custom-call | tf_op jit(solution)/shard_map/weigh/pallas_call | solution.py:210
  311.0 23.6 %update.1 = (f32[2048,1024]{1,0:T(8,128)}, f32[1,2048]{1,0:T(1,128)}, f32[2048,16]{1,0:T(8,128)}) custom-call(f32[2048,1024]{1,0:T(8,128)} %all-gather.5.cloned.1.call-done.rows_ref, bf16[1024,1024]{1,0:T(8,128)(2,1)} %get-tuple-element.31.xh_ref, bf16[1024,1024]{1,0:T(8,128)(2,1)} %get-tuple-element.32.xl_ref, bf16[1024,128]{1,0:T(8,128)(2,1)} %get-tuple-element.33.g_ref, ...), custom_call_target="tpu_custom_call" | custom-call | tf_op jit(solution)/shard_map/update/pallas_call | solution.py:261
  334.6 2.2 copy.26
  (115 shorter events, 40.7 us)
Async XLA Ops:
  7.2 95.0 %reduce-scatter.2.cloned.1.call-start = ((), (), s32[]{:S(2)}) async-start(), calls=%async_computation.1 | async-start | bytes 8912896 | tf_op jit(solution)/shard_map/reduce_scatter | solution.py:340
  16.0 295.0 %all-gather.5.cloned.1.call-start = ((), (), s32[]{:S(2)}) async-start(), calls=%async_computation.2 | async-start | bytes 8912896 | tf_op jit(solution)/shard_map/all_gather | solution.py:368
  17.8 20.4 %collective-permute-start = (f32[512,1024]{1,0:T(8,128)S(1)}, f32[512,1024]{1,0:T(8,128)}, u32[]{:S(2)}, u32[]{:S(2)}) collective-permute-start(f32[512,1024]{1,0:T(8,128)S(1)} %slice.85), channel_id=1, source_target_pairs={{0,16}} | collective-permute-start | bytes 6291464 | tf_op jit(solution)/shard_map/ppermute | solution.py:346
  42.2 20.3 %collective-permute-start.3 = (f32[128,1024]{1,0:T(8,128)}, f32[128,1024]{1,0:T(8,128)S(1)}, u32[]{:S(2)}, u32[]{:S(2)}) collective-permute-start(f32[128,1024]{1,0:T(8,128)} %get-tuple-element.63), channel_id=1, source_target_pairs={{0,1},{16,20}} | collective-permute-start | bytes 1572872 | tf_op jit(solution)/shard_map/ppermute | solution.py:291
  45.4 30.8 %collective-permute-start.2 = (f32[128,1024]{1,0:T(8,128)}, f32[128,1024]{1,0:T(8,128)}, u32[]{:S(2)}, u32[]{:S(2)}) collective-permute-start(f32[128,1024]{1,0:T(8,128)} %get-tuple-element.64), channel_id=1, source_target_pairs={{0,2},{16,24}} | collective-permute-start | bytes 1572872 | tf_op jit(solution)/shard_map/ppermute | solution.py:291
  47.5 28.7 %collective-permute-start.1 = (f32[128,1024]{1,0:T(8,128)S(1)}, f32[128,1024]{1,0:T(8,128)}, u32[]{:S(2)}, u32[]{:S(2)}) collective-permute-start(f32[128,1024]{1,0:T(8,128)S(1)} %get-tuple-element.65), channel_id=1, source_target_pairs={{0,3},{16,28}} | collective-permute-start | bytes 1572872 | tf_op jit(solution)/shard_map/ppermute | solution.py:291
  76.4 3.9 %collective-permute-start.6 = (f32[32,1024]{1,0:T(8,128)S(1)}, f32[32,1024]{1,0:T(8,128)S(1)}, u32[]{:S(2)}, u32[]{:S(2)}) collective-permute-start(f32[32,1024]{1,0:T(8,128)S(1)} %get-tuple-element.66), channel_id=1, source_target_pairs={{0,4},{1,5},{2,6},{3,7},{16,17},{20,21},{24,25},{28,29}} | collective-permute-start | bytes 393224 | tf_op jit(solution)/shard_map/ppermute | solution.py:297
  77.7 3.4 collective-permute-start.5
  79.0 3.2 collective-permute-start.4
  82.2 3.9 %collective-permute-start.9 = (f32[32,1024]{1,0:T(8,128)S(1)}, f32[32,1024]{1,0:T(8,128)S(1)}, u32[]{:S(2)}, u32[]{:S(2)}) collective-permute-start(f32[32,1024]{1,0:T(8,128)S(1)} %fusion.5), channel_id=1, source_target_pairs={{0,32},{4,36},{8,40},{12,44},{1,33},{5,37},{9,41},{13,45},{2,34},{... | collective-permute-start | bytes 393224 | tf_op jit(solution)/shard_map/ppermute | solution.py:301
  83.6 3.8 %collective-permute-start.8 = (f32[32,1024]{1,0:T(8,128)S(1)}, f32[32,1024]{1,0:T(8,128)S(1)}, u32[]{:S(2)}, u32[]{:S(2)}) collective-permute-start(f32[32,1024]{1,0:T(8,128)S(1)} %fusion.5), channel_id=1, source_target_pairs={{0,64},{4,68},{8,72},{12,76},{1,65},{5,69},{9,73},{13,77},{2,66},{... | collective-permute-start | bytes 393224 | tf_op jit(solution)/shard_map/ppermute | solution.py:301
  84.9 3.2 collective-permute-start.7
  88.2 5.7 %collective-permute-start.10 = (f32[32,1024]{1,0:T(8,128)S(1)}, f32[32,1024]{1,0:T(8,128)S(1)}, u32[]{:S(2)}, u32[]{:S(2)}) collective-permute-start(f32[32,1024]{1,0:T(8,128)S(1)} %get-tuple-element.62), channel_id=1, source_target_pairs={{0,4},{4,8},{8,12},{12,0},{1,5},{5,9},{9,13},{13,1},{2,6},{6,10},{... | collective-permute-start | bytes 393224 | tf_op jit(solution)/shard_map/ppermute | solution.py:308
  88.3 12.3 %collective-permute-start.11 = (f32[32,1024]{1,0:T(8,128)S(1)}, f32[32,1024]{1,0:T(8,128)S(1)}, u32[]{:S(2)}, u32[]{:S(2)}) collective-permute-start(f32[32,1024]{1,0:T(8,128)S(1)} %get-tuple-element.62), channel_id=1, source_target_pairs={{0,8},{4,12},{8,0},{12,4},{1,9},{5,13},{9,1},{13,5},{2,10},{6,14},... | collective-permute-start | bytes 393224 | tf_op jit(solution)/shard_map/ppermute | solution.py:308
  92.5 8.0 %collective-permute-start.12 = (f32[32,1024]{1,0:T(8,128)S(1)}, f32[32,1024]{1,0:T(8,128)S(1)}, u32[]{:S(2)}, u32[]{:S(2)}) collective-permute-start(f32[32,1024]{1,0:T(8,128)S(1)} %get-tuple-element.62), channel_id=1, source_target_pairs={{0,12},{4,0},{8,4},{12,8},{1,13},{5,1},{9,5},{13,9},{2,14},{6,2},{... | collective-permute-start | bytes 393224 | tf_op jit(solution)/shard_map/ppermute | solution.py:308
  122.0 14.1 %collective-permute-start.17 = (f32[128,1024]{1,0:T(8,128)S(1)}, f32[128,1024]{1,0:T(8,128)S(1)}, u32[]{:S(2)}, u32[]{:S(2)}) collective-permute-start(f32[128,1024]{1,0:T(8,128)S(1)} %bitcast.49), channel_id=1, source_target_pairs={{0,1},{4,5},{8,9},{12,13},{1,2},{5,6},{9,10},{13,14},{2,3},{6,7},{... | collective-permute-start | bytes 1572872 | tf_op jit(solution)/shard_map/ppermute | solution.py:308
  122.6 19.1 %collective-permute-start.18 = (f32[128,1024]{1,0:T(8,128)S(1)}, f32[128,1024]{1,0:T(8,128)S(1)}, u32[]{:S(2)}, u32[]{:S(2)}) collective-permute-start(f32[128,1024]{1,0:T(8,128)S(1)} %bitcast.50), channel_id=1, source_target_pairs={{0,2},{4,6},{8,10},{12,14},{1,3},{5,7},{9,11},{13,15},{2,0},{6,4},... | collective-permute-start | bytes 1572872 | tf_op jit(solution)/shard_map/ppermute | solution.py:308
  125.5 16.3 %collective-permute-start.19 = (f32[128,1024]{1,0:T(8,128)S(1)}, f32[128,1024]{1,0:T(8,128)S(1)}, u32[]{:S(2)}, u32[]{:S(2)}) collective-permute-start(f32[128,1024]{1,0:T(8,128)S(1)} %bitcast.51), channel_id=1, source_target_pairs={{0,3},{4,7},{8,11},{12,15},{1,0},{5,4},{9,8},{13,12},{2,1},{6,5},{... | collective-permute-start | bytes 1572872 | tf_op jit(solution)/shard_map/ppermute | solution.py:308
  141.8 91.4 %collective-permute-start.20 = (f32[512,1024]{1,0:T(8,128)S(1)}, f32[512,1024]{1,0:T(8,128)}, u32[]{:S(2)}, u32[]{:S(2)}) collective-permute-start(f32[512,1024]{1,0:T(8,128)S(1)} %bitcast.46), channel_id=1, source_target_pairs={{0,16},{16,0},{1,17},{17,1},{2,18},{18,2},{3,19},{19,3},{4,20},{20... | collective-permute-start | bytes 6291464 | tf_op jit(solution)/shard_map/ppermute | solution.py:379
  146.9 55.5 %collective-permute-start.13 = (f32[128,1024]{1,0:T(8,128)}, f32[128,1024]{1,0:T(8,128)}, u32[]{:S(2)}, u32[]{:S(2)}) collective-permute-start(f32[128,1024]{1,0:T(8,128)} %reduce-scatter.2.cloned.1.call-done), channel_id=1, source_target_pairs={{0,0},{1,16},{2,32},{3,48},{4,64},{5,80},{6,96},{7,112},{8,1},{9,1... | collective-permute-start | bytes 1572872 | tf_op jit(solution)/shard_map/ppermute | solution.py:369
  202.4 10.5 %collective-permute-start.16 = (f32[128,1024]{1,0:T(8,128)}, f32[128,1024]{1,0:T(8,128)S(1)}, u32[]{:S(2)}, u32[]{:S(2)}) collective-permute-start(f32[128,1024]{1,0:T(8,128)} %collective-permute-done.13), channel_id=1, source_target_pairs={{0,96},{32,0},{64,32},{96,64},{1,97},{33,1},{65,33},{97,65},{2,98}... | collective-permute-start | bytes 1572872 | tf_op jit(solution)/shard_map/ppermute | solution.py:374
  203.4 11.4 %collective-permute-start.15 = (f32[128,1024]{1,0:T(8,128)}, f32[128,1024]{1,0:T(8,128)}, u32[]{:S(2)}, u32[]{:S(2)}) collective-permute-start(f32[128,1024]{1,0:T(8,128)} %collective-permute-done.13), channel_id=1, source_target_pairs={{0,64},{32,96},{64,0},{96,32},{1,65},{33,97},{65,1},{97,33},{2,66}... | collective-permute-start | bytes 1572872 | tf_op jit(solution)/shard_map/ppermute | solution.py:374
  203.7 26.6 %collective-permute-start.14 = (f32[128,1024]{1,0:T(8,128)}, f32[128,1024]{1,0:T(8,128)}, u32[]{:S(2)}, u32[]{:S(2)}) collective-permute-start(f32[128,1024]{1,0:T(8,128)} %collective-permute-done.13), channel_id=1, source_target_pairs={{0,32},{32,64},{64,96},{96,0},{1,33},{33,65},{65,97},{97,1},{2,34}... | collective-permute-start | bytes 1572872 | tf_op jit(solution)/shard_map/ppermute | solution.py:374
  278.8 6.8 %collective-permute-start.21 = (f32[4,128,1024]{2,1,0:T(8,128)}, f32[4,128,1024]{2,1,0:T(8,128)S(1)}, u32[]{:S(2)}, u32[]{:S(2)}) collective-permute-start(f32[4,128,1024]{2,1,0:T(8,128)} %pad_maximum_fusion.own_ref), channel_id=1, source_target_pairs={{0,16},{16,0},{1,17},{17,1},{2,18},{18,2},{3,19},{19,3},{4,20},{20... | collective-permute-start | bytes 6291464 | tf_op jit(solution)/shard_map/ppermute | solution.py:383
  (7 other events, 120.7 us)
Sparse Core Ops, SparseCore 0:
  16.1 86.0 reduce-scatter.1
  104.3 98.1 all-gather.4
where the time goes:
time: 344 us
  Pallas kernels  93.3 us (27%)
  blocking collectives  86.8 us (25%)
  waiting for transfers between devices  79.8 us (23%)
  starting transfers between devices  30.3 us (9%)
  other arithmetic  27.2 us (8%)
  between operations  15.3 us (4%)
  local copies, waits for them, and re-layouts  11 us (3%)
    pallas_call x1, Pallas kernels, chol_part(): pl.pallas_call(kernel, out_shape=[jax.ShapeDtypeStruct((n, n), jnp.float3...  45.6 us
    all_gather x1, blocking collectives, on_device(): lines = lax.all_gather(lines, ROW, axis=0, tiled=True)  34.2 us
    ppermute x3, waiting for transfers between devices, spread_lead(): lax.ppermute(loads[k], ALL, [(place(0, c, 0, 0), place(0, c, k, 0)) for c...  26.6 us
    ppermute x3, waiting for transfers between devices, on_device(): lax.ppermute(moved, 'y', [(v, (v + k) % 4) for v in range(4)])  24.6 us
    pallas_call x1, Pallas kernels, weigh(): pl.pallas_call(factor_kernel, out_shape=[jax.ShapeDtypeStruct((n, n), jnp...  24.1 us
    pallas_call x1, Pallas kernels, update(): pl.pallas_call(update_kernel, grid=(m // block,), out_shape=[jax.ShapeDty...  23.6 us
    ppermute x6, waiting for transfers between devices, exchange(): got = lax.ppermute(block, ALL, ahead(k))  23.2 us
    all_gather x1, blocking collectives, on_device(): small = lax.all_gather(small, COL, axis=0, tiled=True)  19.1 us
  transfers between devices with their start and end apart: 24, of which 14 were waited for; matrix products, arithmetic and copies ran while one was open for 8% of the time, Pallas kernels for 20%

commit v1 on v0

--- a/solution.py
+++ b/solution.py
@@ -167,17 +167,18 @@
     ri = lax.broadcasted_iota(jnp.int32, (wide, n), 0)
     ci = lax.broadcasted_iota(jnp.int32, (wide, n), 1)
     part = lambda i: pl.ds(pl.multiple_of(i * wide, wide), wide)
+    deep = lambda i: pl.ds(pl.multiple_of(i * 2 * wide, 2 * wide), 2 * wide)
 
     def first(i, _):
         acc[...] = jnp.zeros_like(acc)
 
         def add(k, _):
-            w = split2(w_ref[part(i), part(k)])
-            acc[:, :n] += dot3(w, (ah[:, part(k)], al[:, part(k)]), NT)
-            acc[:, n:] += dot3(w, split2(e_ref[part(k), :]), NN)
+            w = split2(w_ref[part(i), deep(k)])
+            acc[:, :n] += dot3(w, (ah[:, deep(k)], al[:, deep(k)]), NT)
+            acc[:, n:] += dot3(w, split2(e_ref[deep(k), :]), NN)
             return 0
 
-        lax.fori_loop(0, i + 1, add, 0)
+        lax.fori_loop(0, i // 2 + 1, add, 0)
         m = acc[:, :n]
         m = jnp.where(col == 0, jnp.where(ri + i * wide == ci, -1.0, 0.0), m)
         mh[part(i), :n], ml[part(i), :n] = split2(m)
@@ -190,11 +191,11 @@
         acc[...] = jnp.zeros_like(acc)
 
         def add(k, _):
-            w = split2(w_ref[part(k), part(i)].T)
-            acc[...] += dot3(w, (mh[part(k), :], ml[part(k), :]), NN)
+            w = split2(w_ref[deep(k), part(i)].T)
+            acc[...] += dot3(w, (mh[deep(k), :], ml[deep(k), :]), NN)
             return 0
 
-        lax.fori_loop(i, n // wide, add, 0)
+        lax.fori_loop(i // 2, n // (2 * wide), add, 0)
         xh_ref[part(i), :], xl_ref[part(i), :] = split2(acc[:, :n])
         gh, gl = split2(acc[:, n:])
         g_ref[part(i), :64], g_ref[part(i), 64:] = gh[:, :64], gl[:, :64]
@@ -253,7 +254,7 @@
 
 def update(rows, xh, xl, g, covariance, lower, extra, head, diag, sectors):
     m, n = covariance.shape
-    block = 512
+    block = 256
     last = LEAD // block - 1
     whole = lambda a: pl.BlockSpec(a.shape, lambda i: (0, 0))
     lines = lambda w: pl.BlockSpec((block, w), lambda i: (i, 0))

time: 344 us -> 344 us (level)
  no operation moved by 1% of the time
where the time goes in v1:
time: 344 us; the launch traced here: 343 us
  Pallas kernels  93.1 us (27%)
  blocking collectives  86.8 us (25%)
  waiting for transfers between devices  79.8 us (23%)
  starting transfers between devices  30.3 us (9%)
  other arithmetic  27.2 us (8%)
  between operations  15.3 us (4%)
  local copies, waits for them, and re-layouts  11 us (3%)
    pallas_call x1, Pallas kernels, chol_part(): pl.pallas_call(kernel, out_shape=[jax.ShapeDtypeStruct((n, n), jnp.float3...  45.6 us
    all_gather x1, blocking collectives, on_device(): lines = lax.all_gather(lines, ROW, axis=0, tiled=True)  34.2 us
    ppermute x3, waiting for transfers between devices, spread_lead(): lax.ppermute(loads[k], ALL, [(place(0, c, 0, 0), place(0, c, k, 0)) for c...  26.6 us
    ppermute x3, waiting for transfers between devices, on_device(): lax.ppermute(moved, 'y', [(v, (v + k) % 4) for v in range(4)])  24.6 us
    pallas_call x1, Pallas kernels, weigh(): pl.pallas_call(factor_kernel, out_shape=[jax.ShapeDtypeStruct((n, n), jnp...  24.1 us
    pallas_call x1, Pallas kernels, update(): pl.pallas_call(update_kernel, grid=(m // block,), out_shape=[jax.ShapeDty...  23.3 us
    ppermute x6, waiting for transfers between devices, exchange(): got = lax.ppermute(block, ALL, ahead(k))  23.2 us
    all_gather x1, blocking collectives, on_device(): small = lax.all_gather(small, COL, axis=0, tiled=True)  19.1 us
  transfers between devices with their start and end apart: 24, of which 14 were waited for; matrix products, arithmetic and copies ran while one was open for 8% of the time, Pallas kernels for 20%

profile of v1, /device:TPU:1, one launch (start us, length us, event | category | flops | bytes accessed | tf_op | source)
XLA Modules:
  0.0 343.4 jit_solution(2135903344013009328)
XLA Ops:
  7.3 8.7 %broadcast_select_fusion = f32[2048,1024]{1,0:T(8,128)} fusion(f32[2048,1024]{1,0:T(8,128)} %cov_ref.1, pred[]{:T(512)S(6)} %eq.45), kind=kLoop, calls=%fused_computation.5 | loop fusion | flops 2097152 | bytes 16777216 | tf_op jit(solution)/shard_map/jit(_where)/select_n | solution.py:339
  19.1 19.1 %all-gather.2 = f32[16,3,128]{2,1,0:T(4,128)S(1)} all-gather(f32[1,3,128]{2,1,0:T(4,128)S(1)} %bitcast.70), channel_id=1, replica_groups=mesh['y'=4,'core'=2,'z'=4,'x'=4] {'z','x'}, dimensions={0}, use_global_device_ids=true | all-gather | bytes 26112 | tf_op jit(solution)/shard_map/all_gather | solution.py:342
  38.2 3.0 slice_select_fusion
  42.2 3.1 collective-permute-start.3
  47.5 2.1 collective-permute-start.1
  49.6 12.9 %collective-permute-done.3 = f32[128,1024]{1,0:T(8,128)S(1)} collective-permute-done((f32[128,1024]{1,0:T(8,128)}, f32[128,1024]{1,0:T(8,128)S(1)}, u32[]{:S(2)}, u32[]{:S(2)}) %collective-permute-start.3) | collective-permute-done | bytes 524320 | tf_op jit(solution)/shard_map/ppermute | solution.py:292
  62.6 13.6 %collective-permute-done.2 = f32[128,1024]{1,0:T(8,128)} collective-permute-done((f32[128,1024]{1,0:T(8,128)}, f32[128,1024]{1,0:T(8,128)}, u32[]{:S(2)}, u32[]{:S(2)}) %collective-permute-start.2) | collective-permute-done | bytes 524320 | tf_op jit(solution)/shard_map/ppermute | solution.py:292
  88.3 4.2 %collective-permute-start.11 = (f32[32,1024]{1,0:T(8,128)S(1)}, f32[32,1024]{1,0:T(8,128)S(1)}, u32[]{:S(2)}, u32[]{:S(2)}) collective-permute-start(f32[32,1024]{1,0:T(8,128)S(1)} %get-tuple-element.62), channel_id=1, source_target_pairs={{0,8},{4,12},{8,0},{12,4},{1,9},{5,13},{9,1},{13,5},{2,10},{6,14},... | collective-permute-start | bytes 393224 | tf_op jit(solution)/shard_map/ppermute | solution.py:309
  93.9 6.6 %collective-permute-done.11 = f32[32,1024]{1,0:T(8,128)S(1)} collective-permute-done((f32[32,1024]{1,0:T(8,128)S(1)}, f32[32,1024]{1,0:T(8,128)S(1)}, u32[]{:S(2)}, u32[]{:S(2)}) %collective-permute-start.11) | collective-permute-done | bytes 131104 | tf_op jit(solution)/shard_map/ppermute | solution.py:309
  106.2 15.7 %all_gather.17 = f32[384,128]{1,0:T(8,128)S(1)} all-gather(f32[48,128]{1,0:T(8,128)S(1)} %reshape.141), channel_id=1, replica_groups=mesh['y'=4,'core'=2,'z'=4,'x'=4] {'y','core'}, dimensions={0}, use_global_device_ids=true | all-gather | bytes 221184 | tf_op jit(solution)/shard_map/all_gather | solution.py:352
  122.6 2.2 collective-permute-start.18
  126.4 9.8 %collective-permute-done.17 = f32[128,1024]{1,0:T(8,128)S(1)} collective-permute-done((f32[128,1024]{1,0:T(8,128)S(1)}, f32[128,1024]{1,0:T(8,128)S(1)}, u32[]{:S(2)}, u32[]{:S(2)}) %collective-permute-start.17) | collective-permute-done | bytes 524320 | tf_op jit(solution)/shard_map/ppermute | solution.py:309
  136.2 5.5 %collective-permute-done.18 = f32[128,1024]{1,0:T(8,128)S(1)} collective-permute-done((f32[128,1024]{1,0:T(8,128)S(1)}, f32[128,1024]{1,0:T(8,128)S(1)}, u32[]{:S(2)}, u32[]{:S(2)}) %collective-permute-start.18) | collective-permute-done | bytes 524320 | tf_op jit(solution)/shard_map/ppermute | solution.py:309
  142.2 4.7 %multiply_reduce_fusion = (f32[1024]{0:T(1024)S(1)}, f32[2048]{0:T(1024)S(1)}) fusion(f32[2048,1024]{1,0:T(8,128)} %cov_ref.1, f32[2048]{0:T(1024)S(1)} %dynamic_slice.24, s32[1024]{0:T(1024)S(1)} %iota_add_fusion.1, s32[2048]{0:T(1024)S(1)} %iota_add_fusion, f32[1024]{0:T(1024)S(1)} %get-tuple-element.58), kind=kLoop, calls=%fused_computation.3 | loop fusion | flops 16774144 | bytes 8425472 | tf_op jit(solution)/shard_map/reduce_sum | solution.py:358
  146.9 3.3 collective-permute-start.13
  150.2 34.2 %all-gather = f32[16384]{0:T(1024)S(1)} all-gather(f32[2048]{0:T(1024)S(1)} %pad_maximum_fusion.2), channel_id=2, replica_groups=mesh['y'=4,'core'=2,'z'=4,'x'=4] {'y','core'}, dimensions={0}, use_global_device_ids=true | all-gather | bytes 73728 | tf_op jit(solution)/shard_map/all_gather | solution.py:360
  184.5 17.8 %all-gather.1 = f32[49152]{0:T(1024)S(1)} all-gather(f32[3072]{0:T(1024)S(1)} %pad_maximum_fusion.1), channel_id=3, replica_groups=mesh['y'=4,'core'=2,'z'=4,'x'=4] {'z','x'}, dimensions={0}, use_global_device_ids=true | all-gather | bytes 208896 | tf_op jit(solution)/shard_map/all_gather | solution.py:366
  205.7 7.1 %collective-permute-done.16 = f32[128,1024]{1,0:T(8,128)S(1)} collective-permute-done((f32[128,1024]{1,0:T(8,128)}, f32[128,1024]{1,0:T(8,128)S(1)}, u32[]{:S(2)}, u32[]{:S(2)}) %collective-permute-start.16) | collective-permute-done | bytes 524320 | tf_op jit(solution)/shard_map/ppermute | solution.py:375
  214.8 15.5 %collective-permute-done.14 = f32[128,1024]{1,0:T(8,128)} collective-permute-done((f32[128,1024]{1,0:T(8,128)}, f32[128,1024]{1,0:T(8,128)}, u32[]{:S(2)}, u32[]{:S(2)}) %collective-permute-start.14) | collective-permute-done | bytes 524320 | tf_op jit(solution)/shard_map/ppermute | solution.py:375
  230.3 2.9 pad_maximum_fusion.own_ref
  233.2 45.6 %shard_map.102 = (f32[1024,1024]{1,0:T(8,128)}, f32[1024,1024]{1,0:T(8,128)}) custom-call(f32[512,1024]{1,0:T(8,128)S(1)} %bitcast.47, f32[512,1024]{1,0:T(8,128)} %collective-permute-done.20.other_ref, f32[8,128]{1,0:T(8,128)S(1)} %fusion.10.diag_ref), custom_call_target="tpu_custom_call" | custom-call | tf_op jit(solution)/shard_map/pallas_call | solution.py:142
  286.9 24.1 %weigh.1 = (bf16[1024,1024]{1,0:T(8,128)(2,1)}, bf16[1024,1024]{1,0:T(8,128)(2,1)}, bf16[1024,128]{1,0:T(8,128)(2,1)}, f32[1024,128]{1,0:T(8,128)}) custom-call(f32[1024,1024]{1,0:T(8,128)} %get-tuple-element.29.w_ref, f32[4,128,1024]{2,1,0:T(8,128)} %pad_maximum_fusion.own_ref, f32[4,128,1024]{2,1,0:T(8,128)} %copy-done.1, ...), custom_call_target="tpu_custom_call" | custom-call | tf_op jit(solution)/shard_map/weigh/pallas_call | solution.py:211
  311.0 23.3 %update.1 = (f32[2048,1024]{1,0:T(8,128)}, f32[1,2048]{1,0:T(1,128)}, f32[2048,16]{1,0:T(8,128)}) custom-call(f32[2048,1024]{1,0:T(8,128)} %all-gather.5.cloned.1.call-done.rows_ref, bf16[1024,1024]{1,0:T(8,128)(2,1)} %get-tuple-element.31.xh_ref, bf16[1024,1024]{1,0:T(8,128)(2,1)} %get-tuple-element.32.xl_ref, bf16[1024,128]{1,0:T(8,128)(2,1)} %get-tuple-element.33.g_ref, ...), custom_call_target="tpu_custom_call" | custom-call | tf_op jit(solution)/shard_map/update/pallas_call | solution.py:262
  334.4 2.2 copy.26
  (115 shorter events, 40.7 us)
Async XLA Ops:
  7.2 95.0 %reduce-scatter.2.cloned.1.call-start = ((), (), s32[]{:S(2)}) async-start(), calls=%async_computation.1 | async-start | bytes 8912896 | tf_op jit(solution)/shard_map/reduce_scatter | solution.py:341
  16.0 295.0 %all-gather.5.cloned.1.call-start = ((), (), s32[]{:S(2)}) async-start(), calls=%async_computation.2 | async-start | bytes 8912896 | tf_op jit(solution)/shard_map/all_gather | solution.py:369
  17.8 20.4 %collective-permute-start = (f32[512,1024]{1,0:T(8,128)S(1)}, f32[512,1024]{1,0:T(8,128)}, u32[]{:S(2)}, u32[]{:S(2)}) collective-permute-start(f32[512,1024]{1,0:T(8,128)S(1)} %slice.85), channel_id=1, source_target_pairs={{0,16}} | collective-permute-start | bytes 6291464 | tf_op jit(solution)/shard_map/ppermute | solution.py:347
  42.2 20.3 %collective-permute-start.3 = (f32[128,1024]{1,0:T(8,128)}, f32[128,1024]{1,0:T(8,128)S(1)}, u32[]{:S(2)}, u32[]{:S(2)}) collective-permute-start(f32[128,1024]{1,0:T(8,128)} %get-tuple-element.63), channel_id=1, source_target_pairs={{0,1},{16,20}} | collective-permute-start | bytes 1572872 | tf_op jit(solution)/shard_map/ppermute | solution.py:292
  45.4 30.8 %collective-permute-start.2 = (f32[128,1024]{1,0:T(8,128)}, f32[128,1024]{1,0:T(8,128)}, u32[]{:S(2)}, u32[]{:S(2)}) collective-permute-start(f32[128,1024]{1,0:T(8,128)} %get-tuple-element.64), channel_id=1, source_target_pairs={{0,2},{16,24}} | collective-permute-start | bytes 1572872 | tf_op jit(solution)/shard_map/ppermute | solution.py:292
  47.5 28.7 %collective-permute-start.1 = (f32[128,1024]{1,0:T(8,128)S(1)}, f32[128,1024]{1,0:T(8,128)}, u32[]{:S(2)}, u32[]{:S(2)}) collective-permute-start(f32[128,1024]{1,0:T(8,128)S(1)} %get-tuple-element.65), channel_id=1, source_target_pairs={{0,3},{16,28}} | collective-permute-start | bytes 1572872 | tf_op jit(solution)/shard_map/ppermute | solution.py:292
  76.4 3.9 %collective-permute-start.6 = (f32[32,1024]{1,0:T(8,128)S(1)}, f32[32,1024]{1,0:T(8,128)S(1)}, u32[]{:S(2)}, u32[]{:S(2)}) collective-permute-start(f32[32,1024]{1,0:T(8,128)S(1)} %get-tuple-element.66), channel_id=1, source_target_pairs={{0,4},{1,5},{2,6},{3,7},{16,17},{20,21},{24,25},{28,29}} | collective-permute-start | bytes 393224 | tf_op jit(solution)/shard_map/ppermute | solution.py:298
  77.7 3.4 collective-permute-start.5
  79.0 3.2 collective-permute-start.4
  82.2 3.9 %collective-permute-start.9 = (f32[32,1024]{1,0:T(8,128)S(1)}, f32[32,1024]{1,0:T(8,128)S(1)}, u32[]{:S(2)}, u32[]{:S(2)}) collective-permute-start(f32[32,1024]{1,0:T(8,128)S(1)} %fusion.5), channel_id=1, source_target_pairs={{0,32},{4,36},{8,40},{12,44},{1,33},{5,37},{9,41},{13,45},{2,34},{... | collective-permute-start | bytes 393224 | tf_op jit(solution)/shard_map/ppermute | solution.py:302
  83.6 3.8 %collective-permute-start.8 = (f32[32,1024]{1,0:T(8,128)S(1)}, f32[32,1024]{1,0:T(8,128)S(1)}, u32[]{:S(2)}, u32[]{:S(2)}) collective-permute-start(f32[32,1024]{1,0:T(8,128)S(1)} %fusion.5), channel_id=1, source_target_pairs={{0,64},{4,68},{8,72},{12,76},{1,65},{5,69},{9,73},{13,77},{2,66},{... | collective-permute-start | bytes 393224 | tf_op jit(solution)/shard_map/ppermute | solution.py:302
  84.9 3.2 collective-permute-start.7
  88.2 5.7 %collective-permute-start.10 = (f32[32,1024]{1,0:T(8,128)S(1)}, f32[32,1024]{1,0:T(8,128)S(1)}, u32[]{:S(2)}, u32[]{:S(2)}) collective-permute-start(f32[32,1024]{1,0:T(8,128)S(1)} %get-tuple-element.62), channel_id=1, source_target_pairs={{0,4},{4,8},{8,12},{12,0},{1,5},{5,9},{9,13},{13,1},{2,6},{6,10},{... | collective-permute-start | bytes 393224 | tf_op jit(solution)/shard_map/ppermute | solution.py:309
  88.3 12.3 %collective-permute-start.11 = (f32[32,1024]{1,0:T(8,128)S(1)}, f32[32,1024]{1,0:T(8,128)S(1)}, u32[]{:S(2)}, u32[]{:S(2)}) collective-permute-start(f32[32,1024]{1,0:T(8,128)S(1)} %get-tuple-element.62), channel_id=1, source_target_pairs={{0,8},{4,12},{8,0},{12,4},{1,9},{5,13},{9,1},{13,5},{2,10},{6,14},... | collective-permute-start | bytes 393224 | tf_op jit(solution)/shard_map/ppermute | solution.py:309
  92.5 8.0 %collective-permute-start.12 = (f32[32,1024]{1,0:T(8,128)S(1)}, f32[32,1024]{1,0:T(8,128)S(1)}, u32[]{:S(2)}, u32[]{:S(2)}) collective-permute-start(f32[32,1024]{1,0:T(8,128)S(1)} %get-tuple-element.62), channel_id=1, source_target_pairs={{0,12},{4,0},{8,4},{12,8},{1,13},{5,1},{9,5},{13,9},{2,14},{6,2},{... | collective-permute-start | bytes 393224 | tf_op jit(solution)/shard_map/ppermute | solution.py:309
  122.0 14.1 %collective-permute-start.17 = (f32[128,1024]{1,0:T(8,128)S(1)}, f32[128,1024]{1,0:T(8,128)S(1)}, u32[]{:S(2)}, u32[]{:S(2)}) collective-permute-start(f32[128,1024]{1,0:T(8,128)S(1)} %bitcast.49), channel_id=1, source_target_pairs={{0,1},{4,5},{8,9},{12,13},{1,2},{5,6},{9,10},{13,14},{2,3},{6,7},{... | collective-permute-start | bytes 1572872 | tf_op jit(solution)/shard_map/ppermute | solution.py:309
  122.6 19.1 %collective-permute-start.18 = (f32[128,1024]{1,0:T(8,128)S(1)}, f32[128,1024]{1,0:T(8,128)S(1)}, u32[]{:S(2)}, u32[]{:S(2)}) collective-permute-start(f32[128,1024]{1,0:T(8,128)S(1)} %bitcast.50), channel_id=1, source_target_pairs={{0,2},{4,6},{8,10},{12,14},{1,3},{5,7},{9,11},{13,15},{2,0},{6,4},... | collective-permute-start | bytes 1572872 | tf_op jit(solution)/shard_map/ppermute | solution.py:309
  125.5 16.3 %collective-permute-start.19 = (f32[128,1024]{1,0:T(8,128)S(1)}, f32[128,1024]{1,0:T(8,128)S(1)}, u32[]{:S(2)}, u32[]{:S(2)}) collective-permute-start(f32[128,1024]{1,0:T(8,128)S(1)} %bitcast.51), channel_id=1, source_target_pairs={{0,3},{4,7},{8,11},{12,15},{1,0},{5,4},{9,8},{13,12},{2,1},{6,5},{... | collective-permute-start | bytes 1572872 | tf_op jit(solution)/shard_map/ppermute | solution.py:309
  141.8 91.4 %collective-permute-start.20 = (f32[512,1024]{1,0:T(8,128)S(1)}, f32[512,1024]{1,0:T(8,128)}, u32[]{:S(2)}, u32[]{:S(2)}) collective-permute-start(f32[512,1024]{1,0:T(8,128)S(1)} %bitcast.46), channel_id=1, source_target_pairs={{0,16},{16,0},{1,17},{17,1},{2,18},{18,2},{3,19},{19,3},{4,20},{20... | collective-permute-start | bytes 6291464 | tf_op jit(solution)/shard_map/ppermute | solution.py:380
  146.9 55.5 %collective-permute-start.13 = (f32[128,1024]{1,0:T(8,128)}, f32[128,1024]{1,0:T(8,128)}, u32[]{:S(2)}, u32[]{:S(2)}) collective-permute-start(f32[128,1024]{1,0:T(8,128)} %reduce-scatter.2.cloned.1.call-done), channel_id=1, source_target_pairs={{0,0},{1,16},{2,32},{3,48},{4,64},{5,80},{6,96},{7,112},{8,1},{9,1... | collective-permute-start | bytes 1572872 | tf_op jit(solution)/shard_map/ppermute | solution.py:370
  202.4 10.5 %collective-permute-start.16 = (f32[128,1024]{1,0:T(8,128)}, f32[128,1024]{1,0:T(8,128)S(1)}, u32[]{:S(2)}, u32[]{:S(2)}) collective-permute-start(f32[128,1024]{1,0:T(8,128)} %collective-permute-done.13), channel_id=1, source_target_pairs={{0,96},{32,0},{64,32},{96,64},{1,97},{33,1},{65,33},{97,65},{2,98}... | collective-permute-start | bytes 1572872 | tf_op jit(solution)/shard_map/ppermute | solution.py:375
  203.4 11.4 %collective-permute-start.15 = (f32[128,1024]{1,0:T(8,128)}, f32[128,1024]{1,0:T(8,128)}, u32[]{:S(2)}, u32[]{:S(2)}) collective-permute-start(f32[128,1024]{1,0:T(8,128)} %collective-permute-done.13), channel_id=1, source_target_pairs={{0,64},{32,96},{64,0},{96,32},{1,65},{33,97},{65,1},{97,33},{2,66}... | collective-permute-start | bytes 1572872 | tf_op jit(solution)/shard_map/ppermute | solution.py:375
  203.7 26.6 %collective-permute-start.14 = (f32[128,1024]{1,0:T(8,128)}, f32[128,1024]{1,0:T(8,128)}, u32[]{:S(2)}, u32[]{:S(2)}) collective-permute-start(f32[128,1024]{1,0:T(8,128)} %collective-permute-done.13), channel_id=1, source_target_pairs={{0,32},{32,64},{64,96},{96,0},{1,33},{33,65},{65,97},{97,1},{2,34}... | collective-permute-start | bytes 1572872 | tf_op jit(solution)/shard_map/ppermute | solution.py:375
  278.8 6.8 %collective-permute-start.21 = (f32[4,128,1024]{2,1,0:T(8,128)}, f32[4,128,1024]{2,1,0:T(8,128)S(1)}, u32[]{:S(2)}, u32[]{:S(2)}) collective-permute-start(f32[4,128,1024]{2,1,0:T(8,128)} %pad_maximum_fusion.own_ref), channel_id=1, source_target_pairs={{0,16},{16,0},{1,17},{17,1},{2,18},{18,2},{3,19},{19,3},{4,20},{20... | collective-permute-start | bytes 6291464 | tf_op jit(solution)/shard_map/ppermute | solution.py:384
  (7 other events, 120.7 us)
Sparse Core Ops, SparseCore 0:
  16.1 86.0 reduce-scatter.1
  104.3 98.1 all-gather.4
